TPU v7x, 32 devices: a whole 2x2x4 slice. The times are simulated.
32 devices in a mesh: gz: 2 (over core), row: 4 (over y, x), col: 4 (over z).
Axes of the slice: x: 2, y: 2, z: 4, core: 2. Of those that a mesh axis runs over, the one named last changes fastest.
Arguments:
- rhs_sub: float32 [2, 3, 4, 96, 256], P('gz', None, 'row', 'col'), may hold values from -6 to 6
- rhs_top: float32 [2, 4, 96, 256], P(None, 'row', 'col'), may hold values from -6 to 6
- lower_sub: bfloat16 [2, 3, 4, 4, 256, 256], P('gz', None, 'row', 'col'), may hold values from -0.078125 to 0.078125
- lower_link: bfloat16 [2, 2, 4, 4, 256, 256], P('gz', None, 'row', 'col'), may hold values from -0.078125 to 0.078125
- lower_top: bfloat16 [1, 4, 4, 256, 256], P(None, 'row', 'col'), may hold values from -0.078125 to 0.078125
- inv_sub: bfloat16 [2, 3, 4, 256, 256], P('gz', None, 'row'), may hold values from -0.3 to 1.3
- inv_top: bfloat16 [2, 4, 256, 256], P(None, 'row'), may hold values from -0.3 to 1.3
- mask_sub: int32 [2, 3, 4, 4], P('gz', None, 'row', 'col'), may hold values 0 or 1
- mask_link: int32 [2, 2, 4, 4], P('gz', None, 'row', 'col'), may hold values 0 or 1
- mask_top: int32 [1, 4, 4], P(None, 'row', 'col'), may hold values 0 or 1
Outputs:
- sol_sub: float32 [2, 3, 4, 96, 256], P('gz', None, 'row', 'col')
- sol_top: float32 [2, 4, 96, 256], P(None, 'row', 'col')
All inputs are finite; a program needn't handle non-finite values. No bound on the sum of `mask_sub` or of `mask_link` or of `mask_top` on one device may be relied on, other than what follows from the above.
Results may differ from a plain program's by a relative error of at most 0.02.
Values may be sent and summed in bfloat16 or wider, within the bound.
A program may use at most 64 MiB of HBM per device.

v0:
```python
import jax
import jax.numpy as jnp
from jax import lax
from jax.sharding import PartitionSpec as P


def forward_terms(column_vectors, blocks, pattern):
    product = jnp.einsum(
        "jnb,ijbd->ijnd", column_vectors, blocks, preferred_element_type=jnp.float32
    )
    return jnp.sum(product * pattern.astype(jnp.float32)[:, :, None, None], axis=1)


def backward_terms(row_vectors, blocks, pattern):
    product = jnp.einsum("knd,kjbd->kjnb", row_vectors, blocks, preferred_element_type=jnp.float32)
    return jnp.sum(product * pattern.astype(jnp.float32)[:, :, None, None], axis=0)


def inverse_rows(residual, inverse):
    return jnp.einsum(
        "inb,ibd->ind", residual.astype(jnp.bfloat16), inverse, preferred_element_type=jnp.float32
    )


def inverse_cols(residual, inverse):
    return jnp.einsum(
        "ind,ibd->inb", residual.astype(jnp.bfloat16), inverse, preferred_element_type=jnp.float32
    )


def own_share(values, share_cols):
    return lax.dynamic_slice_in_dim(values, lax.axis_index("col") * share_cols, share_cols, 1)


def level_solve(partial_sum, rhs_local, inverse, gate_value, across_groups):
    share_cols = rhs_local.shape[1]
    col_index = lax.axis_index("col")
    placed = lax.dynamic_update_slice_in_dim(
        jnp.zeros_like(partial_sum), rhs_local * gate_value, col_index * share_cols, 1
    )
    residual = lax.psum((placed - partial_sum).astype(jnp.bfloat16), "col").astype(jnp.float32)
    if across_groups:
        residual = lax.psum(residual.astype(jnp.bfloat16), "gz").astype(jnp.float32)
    result = inverse_rows(residual, inverse)
    return result


def column_vectors(rounded, col_blocks):
    col_index = lax.axis_index("col")
    every_block = lax.all_gather(rounded, "row", axis=0, tiled=True)
    result = lax.dynamic_slice_in_dim(every_block, col_index * col_blocks, col_blocks, 0)
    return result


def back_solve(back_part, solved_rows, inverse, share_cols):
    row_blocks = solved_rows.shape[0]
    summed = lax.psum(back_part.astype(jnp.bfloat16), "row").astype(jnp.float32)
    every_block = lax.all_gather(summed.astype(jnp.bfloat16), "col", axis=0, tiled=True).astype(
        summed.dtype
    )
    own_rows = lax.dynamic_slice_in_dim(
        every_block, lax.axis_index("row") * row_blocks, row_blocks, 0
    )
    answer = inverse_cols(solved_rows - own_rows, inverse)
    share = own_share(answer, share_cols)
    half = answer.astype(jnp.bfloat16)
    return (share, half)


def per_device(
    rhs_sub,
    rhs_top,
    lower_sub,
    lower_link,
    lower_top,
    inv_sub,
    inv_top,
    mask_sub,
    mask_link,
    mask_top,
):
    sub_levels = inv_sub.shape[1]
    top_levels = inv_top.shape[0]
    col_blocks = lower_top.shape[2]
    share_cols = rhs_top.shape[2]
    group_gate = (lax.axis_index("gz") == 0).astype(jnp.float32)
    unit_gate = jnp.float32(1.0)
    row_shape = (inv_top.shape[1], share_cols * lax.axis_size("col"), inv_top.shape[-1])
    column_shape = (col_blocks, row_shape[1], row_shape[2])
    sub_solved = []
    sub_columns = []
    for tier_index in range(sub_levels):
        partial_sum = jnp.zeros(row_shape, jnp.float32)
        for earlier in range(tier_index):
            pair_index = tier_index * (tier_index - 1) // 2 + earlier
            partial_sum = partial_sum + forward_terms(
                sub_columns[earlier], lower_sub[0, pair_index], mask_sub[0, pair_index]
            )
        solved = level_solve(
            partial_sum, rhs_sub[0, tier_index], inv_sub[0, tier_index], unit_gate, False
        )
        sub_solved.append(solved)
        sub_columns.append(column_vectors(solved.astype(jnp.bfloat16), col_blocks))
    top_solved = []
    top_columns = []
    for top_level in range(top_levels):
        partial_sum = forward_terms(
            sub_columns[sub_levels - 1], lower_link[0, top_level], mask_link[0, top_level]
        )
        for earlier in range(top_level):
            pair_index = top_level * (top_level - 1) // 2 + earlier
            partial_sum = partial_sum + group_gate * forward_terms(
                top_columns[earlier], lower_top[pair_index], mask_top[pair_index]
            )
        solved = level_solve(partial_sum, rhs_top[top_level], inv_top[top_level], group_gate, True)
        top_solved.append(solved)
        if top_level + 1 < top_levels:
            top_columns.append(column_vectors(solved.astype(jnp.bfloat16), col_blocks))
    top_share = [None] * top_levels
    top_half = [None] * top_levels
    for top_level in reversed(range(top_levels)):
        if top_level + 1 == top_levels:
            answer = inverse_cols(top_solved[top_level], inv_top[top_level])
            share = own_share(answer, share_cols)
            half = answer.astype(jnp.bfloat16)
        else:
            later_level = 1
            pair_index = later_level * (later_level - 1) // 2 + top_level
            back_part = backward_terms(
                top_half[later_level], lower_top[pair_index], mask_top[pair_index]
            )
            share, half = back_solve(
                back_part, top_solved[top_level], inv_top[top_level], share_cols
            )
        top_share[top_level] = share
        top_half[top_level] = half
    sub_share = [None] * sub_levels
    sub_half = [None] * sub_levels
    for tier_index in reversed(range(sub_levels)):
        back_part = jnp.zeros(column_shape, jnp.float32)
        for later_level in range(tier_index + 1, sub_levels):
            pair_index = later_level * (later_level - 1) // 2 + tier_index
            back_part = back_part + backward_terms(
                sub_half[later_level], lower_sub[0, pair_index], mask_sub[0, pair_index]
            )
        if tier_index == sub_levels - 1:
            for top_level in range(top_levels):
                back_part = back_part + backward_terms(
                    top_half[top_level], lower_link[0, top_level], mask_link[0, top_level]
                )
        share, half = back_solve(
            back_part, sub_solved[tier_index], inv_sub[0, tier_index], share_cols
        )
        sub_share[tier_index] = share
        sub_half[tier_index] = half
    sol_sub = jnp.stack(sub_share)[None]
    sol_top = jnp.stack(top_share)
    return (sol_sub, sol_top)


def solution(mesh):
    return jax.shard_map(
        per_device,
        mesh=mesh,
        in_specs=(
            P("gz", None, "row", "col", None),
            P(None, "row", "col", None),
            P("gz", None, "row", "col", None, None),
            P("gz", None, "row", "col", None, None),
            P(None, "row", "col", None, None),
            P("gz", None, "row", None, None),
            P(None, "row", None, None),
            P("gz", None, "row", "col"),
            P("gz", None, "row", "col"),
            P(None, "row", "col"),
        ),
        out_specs=(P("gz", None, "row", "col", None), P(None, "row", "col", None)),
        check_vma=False,
    )
```

profile of v0, /device:TPU:0, one launch (start us, length us, event | category | flops | bytes accessed | tf_op | source)
XLA Modules:
  0.0 261.6 jit_solution(2911516491720442301)
XLA Ops:
  0.6 0.0 copy-start
  0.6 0.0 copy-start.2
  0.7 0.8 bitcast_dynamic-update-slice_fusion.4
  1.5 21.3 %psum.77 = bf16[96,256]{1,0:T(8,128)(2,1)S(1)} all-reduce(bf16[96,256]{1,0:T(8,128)(2,1)S(1)} %convert_bitcast_fusion), channel_id=1, replica_groups=mesh['gz'=2,'row'=4,'col'=4] {'col'}, use_global_device_ids=true, to_apply=%region_0.0 | all-reduce | flops 24576 | bytes 98304 | tf_op jit(solution)/shard_map/psum | solution.py:41
  22.8 0.0 copy-done.2
  22.8 0.0 copy-start.1
  22.8 0.2 fusion.124
  22.9 8.7 %all-gather = bf16[384,256]{1,0:T(8,128)(2,1)S(1)} all-gather(bf16[96,256]{1,0:T(8,128)(2,1)S(1)} %get-tuple-element.7), channel_id=2, replica_groups=mesh['gz'=2,'row'=4,'col'=4] {'row'}, dimensions={0}, use_global_device_ids=true | all-gather | bytes 245760 | tf_op jit(solution)/shard_map/all_gather | solution.py:50
  31.7 0.0 copy-start.5
  31.7 0.9 copy-done.5
  32.6 0.0 copy-start.7
  32.6 0.6 copy-done.7
  33.2 0.6 fusion.123
  34.5 0.0 copy-done.1
  34.5 0.2 fusion.26
  34.6 16.1 %psum.78 = bf16[96,256]{1,0:T(8,128)(2,1)S(1)} all-reduce(bf16[96,256]{1,0:T(8,128)(2,1)S(1)} %fusion.26), channel_id=1, replica_groups=mesh['gz'=2,'row'=4,'col'=4] {'col'}, use_global_device_ids=true, to_apply=%region_1.0 | all-reduce | flops 24576 | bytes 98304 | tf_op jit(solution)/shard_map/psum | solution.py:41
  50.7 0.2 fusion.125
  50.9 8.7 %all-gather.1 = bf16[384,256]{1,0:T(8,128)(2,1)S(1)} all-gather(bf16[96,256]{1,0:T(8,128)(2,1)S(1)} %get-tuple-element.9), channel_id=3, replica_groups=mesh['gz'=2,'row'=4,'col'=4] {'row'}, dimensions={0}, use_global_device_ids=true | all-gather | bytes 245760 | tf_op jit(solution)/shard_map/all_gather | solution.py:50
  60.2 0.2 convolution_multiply_fusion.9
  61.0 0.2 fusion.27
  61.2 18.0 %psum.79 = bf16[96,256]{1,0:T(8,128)(2,1)S(1)} all-reduce(bf16[96,256]{1,0:T(8,128)(2,1)S(1)} %fusion.27), channel_id=1, replica_groups=mesh['gz'=2,'row'=4,'col'=4] {'col'}, use_global_device_ids=true, to_apply=%region_2.0 | all-reduce | flops 24576 | bytes 98304 | tf_op jit(solution)/shard_map/psum | solution.py:41
  79.2 0.2 fusion.126
  79.4 0.0 copy-start.3
  79.4 7.9 %all-gather.2 = bf16[384,256]{1,0:T(8,128)(2,1)S(1)} all-gather(bf16[96,256]{1,0:T(8,128)(2,1)S(1)} %get-tuple-element.11), channel_id=4, replica_groups=mesh['gz'=2,'row'=4,'col'=4] {'row'}, dimensions={0}, use_global_device_ids=true | all-gather | bytes 245760 | tf_op jit(solution)/shard_map/all_gather | solution.py:50
  87.2 0.0 copy-start.6
  87.2 0.8 copy-done.6
  88.0 0.0 copy-start.8
  88.0 0.6 copy-done.8
  88.7 0.6 fusion.122
  90.0 0.0 copy-done.3
  90.0 0.0 copy-start.4
  90.0 0.2 fusion.17
  90.2 16.1 %psum.80 = bf16[1,96,256]{2,1,0:T(8,128)(2,1)S(1)} all-reduce(bf16[1,96,256]{2,1,0:T(8,128)(2,1)S(1)} %fusion.17), channel_id=1, replica_groups=mesh['gz'=2,'row'=4,'col'=4] {'col'}, use_global_device_ids=true, to_apply=%region_3.0 | all-reduce | flops 24576 | bytes 98304 | tf_op jit(solution)/shard_map/psum | solution.py:41
  106.3 3.5 %psum.81 = bf16[96,256]{1,0:T(8,128)(2,1)S(1)} all-reduce(bf16[96,256]{1,0:T(8,128)(2,1)S(1)} %bitcast.253), channel_id=1, replica_groups=mesh['gz'=2,'row'=4,'col'=4] {'gz'}, use_global_device_ids=true, to_apply=%region_4.0 | all-reduce | flops 24576 | bytes 98304 | tf_op jit(solution)/shard_map/psum | solution.py:43
  109.8 0.0 copy-done.4
  109.8 0.2 fusion.127
  110.0 8.7 %all-gather.3 = bf16[384,256]{1,0:T(8,128)(2,1)S(1)} all-gather(bf16[96,256]{1,0:T(8,128)(2,1)S(1)} %get-tuple-element.13), channel_id=5, replica_groups=mesh['gz'=2,'row'=4,'col'=4] {'row'}, dimensions={0}, use_global_device_ids=true | all-gather | bytes 245760 | tf_op jit(solution)/shard_map/all_gather | solution.py:50
  119.4 0.0 copy-done
  119.4 0.2 fusion.6
  120.2 0.2 fusion.16
  120.4 18.0 %psum.82 = bf16[1,96,256]{2,1,0:T(8,128)(2,1)S(1)} all-reduce(bf16[1,96,256]{2,1,0:T(8,128)(2,1)S(1)} %fusion.16), channel_id=1, replica_groups=mesh['gz'=2,'row'=4,'col'=4] {'col'}, use_global_device_ids=true, to_apply=%region_5.0 | all-reduce | flops 24576 | bytes 98304 | tf_op jit(solution)/shard_map/psum | solution.py:41
  138.4 3.5 %psum.83 = bf16[96,256]{1,0:T(8,128)(2,1)S(1)} all-reduce(bf16[96,256]{1,0:T(8,128)(2,1)S(1)} %bitcast.254), channel_id=1, replica_groups=mesh['gz'=2,'row'=4,'col'=4] {'gz'}, use_global_device_ids=true, to_apply=%region_6.0 | all-reduce | flops 24576 | bytes 98304 | tf_op jit(solution)/shard_map/psum | solution.py:43
  142.0 0.3 fusion.21
  142.3 0.2 fusion.23
  142.5 15.8 %psum.84 = bf16[1,96,256]{2,1,0:T(8,128)(2,1)S(1)} all-reduce(bf16[1,96,256]{2,1,0:T(8,128)(2,1)S(1)} %fusion.23), channel_id=1, replica_groups=mesh['gz'=2,'row'=4,'col'=4] {'row'}, use_global_device_ids=true, to_apply=%region_7.0 | all-reduce | flops 24576 | bytes 98304 | tf_op jit(solution)/shard_map/psum | solution.py:57
  158.3 13.7 %all_gather.28 = bf16[4,96,256]{2,1,0:T(8,128)(2,1)S(1)} all-gather(bf16[1,96,256]{2,1,0:T(8,128)(2,1)S(1)} %psum.84), channel_id=1, replica_groups=mesh['gz'=2,'row'=4,'col'=4] {'col'}, dimensions={0}, use_global_device_ids=true | all-gather | bytes 245760 | tf_op jit(solution)/shard_map/all_gather | solution.py:58
  172.0 0.2 fusion.34
  172.2 0.6 pad_maximum_fusion
  172.8 0.2 convolution_multiply_fusion.3
  173.0 0.2 fusion.24
  173.2 14.7 %psum.85 = bf16[1,96,256]{2,1,0:T(8,128)(2,1)S(1)} all-reduce(bf16[1,96,256]{2,1,0:T(8,128)(2,1)S(1)} %fusion.24), channel_id=1, replica_groups=mesh['gz'=2,'row'=4,'col'=4] {'row'}, use_global_device_ids=true, to_apply=%region_8.0 | all-reduce | flops 24576 | bytes 98304 | tf_op jit(solution)/shard_map/psum | solution.py:57
  187.9 13.6 %all_gather.29 = bf16[4,96,256]{2,1,0:T(8,128)(2,1)S(1)} all-gather(bf16[1,96,256]{2,1,0:T(8,128)(2,1)S(1)} %psum.85), channel_id=1, replica_groups=mesh['gz'=2,'row'=4,'col'=4] {'col'}, dimensions={0}, use_global_device_ids=true | all-gather | bytes 245760 | tf_op jit(solution)/shard_map/all_gather | solution.py:58
  201.5 0.2 fusion.40
  201.7 0.2 fusion.22
  201.9 15.7 %psum.86 = bf16[1,96,256]{2,1,0:T(8,128)(2,1)S(1)} all-reduce(bf16[1,96,256]{2,1,0:T(8,128)(2,1)S(1)} %fusion.22), channel_id=1, replica_groups=mesh['gz'=2,'row'=4,'col'=4] {'row'}, use_global_device_ids=true, to_apply=%region_9.0 | all-reduce | flops 24576 | bytes 98304 | tf_op jit(solution)/shard_map/psum | solution.py:57
  217.6 13.8 %all_gather.30 = bf16[4,96,256]{2,1,0:T(8,128)(2,1)S(1)} all-gather(bf16[1,96,256]{2,1,0:T(8,128)(2,1)S(1)} %psum.86), channel_id=1, replica_groups=mesh['gz'=2,'row'=4,'col'=4] {'col'}, dimensions={0}, use_global_device_ids=true | all-gather | bytes 245760 | tf_op jit(solution)/shard_map/all_gather | solution.py:58
  231.4 0.2 fusion.48
  231.5 0.2 convolution_multiply_fusion
  231.8 0.2 fusion.25
  232.0 15.2 %psum.87 = bf16[1,96,256]{2,1,0:T(8,128)(2,1)S(1)} all-reduce(bf16[1,96,256]{2,1,0:T(8,128)(2,1)S(1)} %fusion.25), channel_id=1, replica_groups=mesh['gz'=2,'row'=4,'col'=4] {'row'}, use_global_device_ids=true, to_apply=%region_10.0 | all-reduce | flops 24576 | bytes 98304 | tf_op jit(solution)/shard_map/psum | solution.py:57
  247.2 13.6 %all_gather.31 = bf16[4,96,256]{2,1,0:T(8,128)(2,1)S(1)} all-gather(bf16[1,96,256]{2,1,0:T(8,128)(2,1)S(1)} %psum.87), channel_id=1, replica_groups=mesh['gz'=2,'row'=4,'col'=4] {'col'}, dimensions={0}, use_global_device_ids=true | all-gather | bytes 245760 | tf_op jit(solution)/shard_map/all_gather | solution.py:58
  260.8 0.2 fusion.54
  261.0 0.6 maximum_bitcast_fusion
  (15 shorter events, 0.2 us)
Async XLA Ops:
  0.6 118.7 %copy-start = (bf16[1,1,1,256,256]{4,3,2,1,0:T(8,128)(2,1)S(1)}, bf16[1,1,1,256,256]{4,3,2,1,0:T(8,128)(2,1)}, u32[]{:S(2)}) copy-start(bf16[1,1,1,256,256]{4,3,2,1,0:T(8,128)(2,1)} %param.14) | copy-start | bytes 393220
  0.6 22.1 %copy-start.2 = (bf16[1,3,1,256,256]{4,3,2,1,0:T(8,128)(2,1)S(1)}, bf16[1,3,1,256,256]{4,3,2,1,0:T(8,128)(2,1)}, u32[]{:S(2)}) copy-start(bf16[1,3,1,256,256]{4,3,2,1,0:T(8,128)(2,1)} %param.15) | copy-start | bytes 1179652
  22.8 11.7 %copy-start.1 = (bf16[1,3,1,1,256,256]{5,4,3,2,1,0:T(8,128)(2,1)S(1)}, bf16[1,3,1,1,256,256]{5,4,3,2,1,0:T(8,128)(2,1)}, u32[]{:S(2)}) copy-start(bf16[1,3,1,1,256,256]{5,4,3,2,1,0:T(8,128)(2,1)} %param.12) | copy-start | bytes 1179652
  31.7 0.9 copy-start.5
  32.6 0.7 copy-start.7
  79.4 10.6 %copy-start.3 = (bf16[1,2,1,1,256,256]{5,4,3,2,1,0:T(8,128)(2,1)S(1)}, bf16[1,2,1,1,256,256]{5,4,3,2,1,0:T(8,128)(2,1)}, u32[]{:S(2)}) copy-start(bf16[1,2,1,1,256,256]{5,4,3,2,1,0:T(8,128)(2,1)} %param.13) | copy-start | bytes 786436
  87.2 0.8 copy-start.6
  88.0 0.7 copy-start.8
  90.0 19.8 %copy-start.4 = (bf16[2,1,256,256]{3,2,1,0:T(8,128)(2,1)S(1)}, bf16[2,1,256,256]{3,2,1,0:T(8,128)(2,1)}, u32[]{:S(2)}) copy-start(bf16[2,1,256,256]{3,2,1,0:T(8,128)(2,1)} %param.16) | copy-start | bytes 786436
where the time goes:
time: 262 us
  blocking collectives  247 us (94%)
  local copies, waits for them, and re-layouts  5.17 us (2%)
  between operations  4.84 us (2%)
  matrix products  3.7 us (1%)
    psum x5, blocking collectives, level_solve(): lax.psum((placed - partial_sum).astype(jnp.bfloat16), 'col')  89.5 us
    psum x4, blocking collectives, back_solve(): summed = lax.psum(back_part.astype(jnp.bfloat16), 'row').astype(jnp.float32)  61.4 us
    all_gather x4, blocking collectives, back_solve(): lax.all_gather(summed.astype(jnp.bfloat16), 'col', axis=0, tiled=True)  54.6 us
    all_gather x4, blocking collectives, column_vectors(): every_block = lax.all_gather(rounded, 'row', axis=0, tiled=True)  34 us
    psum x2, blocking collectives, level_solve(): residual = lax.psum(residual.astype(jnp.bfloat16), 'gz').astype(jnp.float32)  7.06 us

commit v1 on v0

--- a/solution.py
+++ b/solution.py
@@ -54,7 +54,9 @@
 
 def back_solve(back_part, solved_rows, inverse, share_cols):
     row_blocks = solved_rows.shape[0]
-    summed = lax.psum(back_part.astype(jnp.bfloat16), "row").astype(jnp.float32)
+    summed = jnp.sum(lax.all_gather(back_part.astype(jnp.bfloat16), "row"), axis=0).astype(
+        jnp.float32
+    )
     every_block = lax.all_gather(summed.astype(jnp.bfloat16), "col", axis=0, tiled=True).astype(
         summed.dtype
     )

time: 262 us -> 234 us (0.89)
  blocking collectives: 247 us -> 219 us
    psum x4 -> x0, blocking collectives: 61.4 us -> none  [back_solve(): summed = lax.psum(back_part.astype(jnp.bfloat16), 'row').astype(jnp.float32)]
    all_gather x0 -> x4, blocking collectives: none -> 33 us  [back_solve(): lax.all_gather(back_part.astype(jnp.bfloat16), 'row')]
where the time goes in v1:
time: 234 us
  blocking collectives  219 us (94%)
  local copies, waits for them, and re-layouts  5.17 us (2%)
  between operations  4.83 us (2%)
  matrix products  3.71 us (2%)
    psum x5, blocking collectives, level_solve(): lax.psum((placed - partial_sum).astype(jnp.bfloat16), 'col')  89.5 us
    all_gather x4, blocking collectives, back_solve(): lax.all_gather(summed.astype(jnp.bfloat16), 'col', axis=0, tiled=True)  54.9 us
    all_gather x4, blocking collectives, column_vectors(): every_block = lax.all_gather(rounded, 'row', axis=0, tiled=True)  34 us
    all_gather x4, blocking collectives, back_solve(): lax.all_gather(back_part.astype(jnp.bfloat16), 'row')  33 us
    psum x2, blocking collectives, level_solve(): residual = lax.psum(residual.astype(jnp.bfloat16), 'gz').astype(jnp.float32)  7.06 us

profile of v1, /device:TPU:0, one launch (start us, length us, event | category | flops | bytes accessed | tf_op | source)
XLA Modules:
  0.0 233.6 jit_solution(6109636196312260751)
XLA Ops:
  0.6 0.0 copy-start
  0.6 0.0 copy-start.2
  0.7 0.8 bitcast_dynamic-update-slice_fusion.4
  1.5 21.3 %psum.49 = bf16[96,256]{1,0:T(8,128)(2,1)S(1)} all-reduce(bf16[96,256]{1,0:T(8,128)(2,1)S(1)} %convert_bitcast_fusion), channel_id=1, replica_groups=mesh['gz'=2,'row'=4,'col'=4] {'col'}, use_global_device_ids=true, to_apply=%region_0.0 | all-reduce | flops 24576 | bytes 98304 | tf_op jit(solution)/shard_map/psum | solution.py:41
  22.8 0.0 copy-done.2
  22.8 0.0 copy-start.1
  22.8 0.2 fusion.124
  22.9 8.7 %all-gather = bf16[384,256]{1,0:T(8,128)(2,1)S(1)} all-gather(bf16[96,256]{1,0:T(8,128)(2,1)S(1)} %get-tuple-element.7), channel_id=2, replica_groups=mesh['gz'=2,'row'=4,'col'=4] {'row'}, dimensions={0}, use_global_device_ids=true | all-gather | bytes 245760 | tf_op jit(solution)/shard_map/all_gather | solution.py:50
  31.7 0.0 copy-start.5
  31.7 0.9 copy-done.5
  32.6 0.0 copy-start.7
  32.6 0.6 copy-done.7
  33.2 0.6 fusion.123
  34.5 0.0 copy-done.1
  34.5 0.2 fusion.26
  34.6 16.1 %psum.50 = bf16[96,256]{1,0:T(8,128)(2,1)S(1)} all-reduce(bf16[96,256]{1,0:T(8,128)(2,1)S(1)} %fusion.26), channel_id=1, replica_groups=mesh['gz'=2,'row'=4,'col'=4] {'col'}, use_global_device_ids=true, to_apply=%region_1.0 | all-reduce | flops 24576 | bytes 98304 | tf_op jit(solution)/shard_map/psum | solution.py:41
  50.7 0.2 fusion.125
  50.9 8.7 %all-gather.1 = bf16[384,256]{1,0:T(8,128)(2,1)S(1)} all-gather(bf16[96,256]{1,0:T(8,128)(2,1)S(1)} %get-tuple-element.9), channel_id=3, replica_groups=mesh['gz'=2,'row'=4,'col'=4] {'row'}, dimensions={0}, use_global_device_ids=true | all-gather | bytes 245760 | tf_op jit(solution)/shard_map/all_gather | solution.py:50
  60.2 0.2 convolution_multiply_fusion.9
  61.0 0.2 fusion.27
  61.2 18.0 %psum.51 = bf16[96,256]{1,0:T(8,128)(2,1)S(1)} all-reduce(bf16[96,256]{1,0:T(8,128)(2,1)S(1)} %fusion.27), channel_id=1, replica_groups=mesh['gz'=2,'row'=4,'col'=4] {'col'}, use_global_device_ids=true, to_apply=%region_2.0 | all-reduce | flops 24576 | bytes 98304 | tf_op jit(solution)/shard_map/psum | solution.py:41
  79.2 0.2 fusion.126
  79.4 0.0 copy-start.3
  79.4 7.9 %all-gather.2 = bf16[384,256]{1,0:T(8,128)(2,1)S(1)} all-gather(bf16[96,256]{1,0:T(8,128)(2,1)S(1)} %get-tuple-element.11), channel_id=4, replica_groups=mesh['gz'=2,'row'=4,'col'=4] {'row'}, dimensions={0}, use_global_device_ids=true | all-gather | bytes 245760 | tf_op jit(solution)/shard_map/all_gather | solution.py:50
  87.2 0.0 copy-start.6
  87.2 0.8 copy-done.6
  88.0 0.0 copy-start.8
  88.0 0.6 copy-done.8
  88.7 0.6 fusion.122
  90.0 0.0 copy-done.3
  90.0 0.0 copy-start.4
  90.0 0.2 fusion.17
  90.2 16.1 %psum.52 = bf16[1,96,256]{2,1,0:T(8,128)(2,1)S(1)} all-reduce(bf16[1,96,256]{2,1,0:T(8,128)(2,1)S(1)} %fusion.17), channel_id=1, replica_groups=mesh['gz'=2,'row'=4,'col'=4] {'col'}, use_global_device_ids=true, to_apply=%region_3.0 | all-reduce | flops 24576 | bytes 98304 | tf_op jit(solution)/shard_map/psum | solution.py:41
  106.3 3.5 %psum.53 = bf16[96,256]{1,0:T(8,128)(2,1)S(1)} all-reduce(bf16[96,256]{1,0:T(8,128)(2,1)S(1)} %bitcast.249), channel_id=1, replica_groups=mesh['gz'=2,'row'=4,'col'=4] {'gz'}, use_global_device_ids=true, to_apply=%region_4.0 | all-reduce | flops 24576 | bytes 98304 | tf_op jit(solution)/shard_map/psum | solution.py:43
  109.8 0.0 copy-done.4
  109.8 0.2 fusion.127
  110.0 8.7 %all-gather.3 = bf16[384,256]{1,0:T(8,128)(2,1)S(1)} all-gather(bf16[96,256]{1,0:T(8,128)(2,1)S(1)} %get-tuple-element.13), channel_id=5, replica_groups=mesh['gz'=2,'row'=4,'col'=4] {'row'}, dimensions={0}, use_global_device_ids=true | all-gather | bytes 245760 | tf_op jit(solution)/shard_map/all_gather | solution.py:50
  119.4 0.0 copy-done
  119.4 0.2 fusion.6
  120.2 0.2 fusion.16
  120.4 18.0 %psum.54 = bf16[1,96,256]{2,1,0:T(8,128)(2,1)S(1)} all-reduce(bf16[1,96,256]{2,1,0:T(8,128)(2,1)S(1)} %fusion.16), channel_id=1, replica_groups=mesh['gz'=2,'row'=4,'col'=4] {'col'}, use_global_device_ids=true, to_apply=%region_5.0 | all-reduce | flops 24576 | bytes 98304 | tf_op jit(solution)/shard_map/psum | solution.py:41
  138.4 3.5 %psum.55 = bf16[96,256]{1,0:T(8,128)(2,1)S(1)} all-reduce(bf16[96,256]{1,0:T(8,128)(2,1)S(1)} %bitcast.250), channel_id=1, replica_groups=mesh['gz'=2,'row'=4,'col'=4] {'gz'}, use_global_device_ids=true, to_apply=%region_6.0 | all-reduce | flops 24576 | bytes 98304 | tf_op jit(solution)/shard_map/psum | solution.py:43
  142.0 0.3 fusion.21
  142.3 0.2 fusion.23
  142.5 7.7 %all_gather.44 = bf16[4,1,96,256]{3,2,1,0:T(8,128)(2,1)S(1)} all-gather(bf16[1,1,96,256]{3,2,1,0:T(8,128)(2,1)S(1)} %fusion.23), channel_id=1, replica_groups=mesh['gz'=2,'row'=4,'col'=4] {'row'}, dimensions={0}, use_global_device_ids=true | all-gather | bytes 245760 | tf_op jit(solution)/shard_map/all_gather | solution.py:57
  150.2 13.6 %all-gather.4 = bf16[384,256]{1,0:T(8,128)(2,1)S(1)} all-gather(bf16[96,256]{1,0:T(8,128)(2,1)S(1)} %reduce_sum.79), channel_id=6, replica_groups=mesh['gz'=2,'row'=4,'col'=4] {'col'}, dimensions={0}, use_global_device_ids=true | all-gather | bytes 245760 | tf_op jit(solution)/shard_map/all_gather | solution.py:60
  163.8 0.2 fusion.34
  164.1 0.6 pad_maximum_fusion
  164.7 0.2 convolution_multiply_fusion.3
  164.9 0.2 fusion.24
  165.1 8.7 %all_gather.46 = bf16[4,1,96,256]{3,2,1,0:T(8,128)(2,1)S(1)} all-gather(bf16[1,1,96,256]{3,2,1,0:T(8,128)(2,1)S(1)} %fusion.24), channel_id=1, replica_groups=mesh['gz'=2,'row'=4,'col'=4] {'row'}, dimensions={0}, use_global_device_ids=true | all-gather | bytes 245760 | tf_op jit(solution)/shard_map/all_gather | solution.py:57
  173.8 13.7 %all-gather.5 = bf16[384,256]{1,0:T(8,128)(2,1)S(1)} all-gather(bf16[96,256]{1,0:T(8,128)(2,1)S(1)} %reduce_sum.84), channel_id=7, replica_groups=mesh['gz'=2,'row'=4,'col'=4] {'col'}, dimensions={0}, use_global_device_ids=true | all-gather | bytes 245760 | tf_op jit(solution)/shard_map/all_gather | solution.py:60
  187.5 0.2 fusion.40
  187.7 0.2 fusion.22
  187.9 7.7 %all_gather.48 = bf16[4,1,96,256]{3,2,1,0:T(8,128)(2,1)S(1)} all-gather(bf16[1,1,96,256]{3,2,1,0:T(8,128)(2,1)S(1)} %fusion.22), channel_id=1, replica_groups=mesh['gz'=2,'row'=4,'col'=4] {'row'}, dimensions={0}, use_global_device_ids=true | all-gather | bytes 245760 | tf_op jit(solution)/shard_map/all_gather | solution.py:57
  195.7 14.0 %all-gather.6 = bf16[384,256]{1,0:T(8,128)(2,1)S(1)} all-gather(bf16[96,256]{1,0:T(8,128)(2,1)S(1)} %reduce_sum.86), channel_id=8, replica_groups=mesh['gz'=2,'row'=4,'col'=4] {'col'}, dimensions={0}, use_global_device_ids=true | all-gather | bytes 245760 | tf_op jit(solution)/shard_map/all_gather | solution.py:60
  209.7 0.2 fusion.48
  209.8 0.2 convolution_multiply_fusion
  210.1 0.2 fusion.25
  210.3 8.8 %all_gather.50 = bf16[4,1,96,256]{3,2,1,0:T(8,128)(2,1)S(1)} all-gather(bf16[1,1,96,256]{3,2,1,0:T(8,128)(2,1)S(1)} %fusion.25), channel_id=1, replica_groups=mesh['gz'=2,'row'=4,'col'=4] {'row'}, dimensions={0}, use_global_device_ids=true | all-gather | bytes 245760 | tf_op jit(solution)/shard_map/all_gather | solution.py:57
  219.1 13.6 %all-gather.7 = bf16[384,256]{1,0:T(8,128)(2,1)S(1)} all-gather(bf16[96,256]{1,0:T(8,128)(2,1)S(1)} %reduce_sum.91), channel_id=9, replica_groups=mesh['gz'=2,'row'=4,'col'=4] {'col'}, dimensions={0}, use_global_device_ids=true | all-gather | bytes 245760 | tf_op jit(solution)/shard_map/all_gather | solution.py:60
  232.8 0.2 fusion.54
  233.0 0.6 maximum_bitcast_fusion
  (19 shorter events, 0.3 us)
Async XLA Ops:
  0.6 118.7 %copy-start = (bf16[1,1,1,256,256]{4,3,2,1,0:T(8,128)(2,1)S(1)}, bf16[1,1,1,256,256]{4,3,2,1,0:T(8,128)(2,1)}, u32[]{:S(2)}) copy-start(bf16[1,1,1,256,256]{4,3,2,1,0:T(8,128)(2,1)} %param.14) | copy-start | bytes 393220
  0.6 22.1 %copy-start.2 = (bf16[1,3,1,256,256]{4,3,2,1,0:T(8,128)(2,1)S(1)}, bf16[1,3,1,256,256]{4,3,2,1,0:T(8,128)(2,1)}, u32[]{:S(2)}) copy-start(bf16[1,3,1,256,256]{4,3,2,1,0:T(8,128)(2,1)} %param.15) | copy-start | bytes 1179652
  22.8 11.7 %copy-start.1 = (bf16[1,3,1,1,256,256]{5,4,3,2,1,0:T(8,128)(2,1)S(1)}, bf16[1,3,1,1,256,256]{5,4,3,2,1,0:T(8,128)(2,1)}, u32[]{:S(2)}) copy-start(bf16[1,3,1,1,256,256]{5,4,3,2,1,0:T(8,128)(2,1)} %param.12) | copy-start | bytes 1179652
  31.7 0.9 copy-start.5
  32.6 0.7 copy-start.7
  79.4 10.6 %copy-start.3 = (bf16[1,2,1,1,256,256]{5,4,3,2,1,0:T(8,128)(2,1)S(1)}, bf16[1,2,1,1,256,256]{5,4,3,2,1,0:T(8,128)(2,1)}, u32[]{:S(2)}) copy-start(bf16[1,2,1,1,256,256]{5,4,3,2,1,0:T(8,128)(2,1)} %param.13) | copy-start | bytes 786436
  87.2 0.8 copy-start.6
  88.0 0.7 copy-start.8
  90.0 19.8 %copy-start.4 = (bf16[2,1,256,256]{3,2,1,0:T(8,128)(2,1)S(1)}, bf16[2,1,256,256]{3,2,1,0:T(8,128)(2,1)}, u32[]{:S(2)}) copy-start(bf16[2,1,256,256]{3,2,1,0:T(8,128)(2,1)} %param.16) | copy-start | bytes 786436
